TPU v7x, 32 devices: a whole 2x2x4 slice. The times are simulated.
32 devices in a mesh: replica: 4 (over x, core), shard: 8 (over z, y).
Axes of the slice: x: 2, y: 2, z: 4, core: 2. Of those that a mesh axis runs over, the one named last changes fastest.
Arguments:
- block_input: bfloat16 [8192, 2048], P(('replica', 'shard')), may hold values from -6 to 6
- segment_ids: int32 [32, 256], P(('replica', 'shard')), may hold values from 0 to 3, never falling along the last dimension, each value on 1 to 128 neighbouring positions
- attn_gain: bfloat16 [2048], P('shard'), may hold values from 0.5 to 1.5
- mlp_gain: bfloat16 [2048], P('shard'), may hold values from 0.5 to 1.5
- w_query: bfloat16 [2048, 2048], P('shard'), may hold values from -0.125 to 0.125
- w_key: bfloat16 [2048, 2048], P('shard'), may hold values from -0.125 to 0.125
- w_value: bfloat16 [2048, 2048], P('shard'), may hold values from -0.125 to 0.125
- w_out: bfloat16 [2048, 2048], P('shard'), may hold values from -0.5 to 0.5
- w_gate: bfloat16 [2048, 8192], P('shard'), may hold values from -0.125 to 0.125
- w_up: bfloat16 [2048, 8192], P('shard'), may hold values from -0.125 to 0.125
- w_down: bfloat16 [8192, 2048], P('shard'), may hold values from -0.0625 to 0.0625
- out_grad: bfloat16 [8192, 2048], P(('replica', 'shard')), may hold values from -6 to 6
Outputs:
- block_output: bfloat16 [8192, 2048], P(('replica', 'shard'))
- input_grad: float32 [8192, 2048], P(('replica', 'shard'))
- grad_query: float32 [2048, 2048], P('shard')
- grad_key: float32 [2048, 2048], P('shard')
- grad_value: float32 [2048, 2048], P('shard')
- grad_out: float32 [2048, 2048], P('shard')
- grad_gate: float32 [2048, 8192], P('shard')
- grad_up: float32 [2048, 8192], P('shard')
- grad_down: float32 [8192, 2048], P('shard')
- grad_attn_gain: float32 [2048], P('shard')
- grad_mlp_gain: float32 [2048], P('shard')
Inputs may be any that keep to these rules, and one draw needn't show every extreme that they name: `segment_ids`: along each packed row the ids never fall; every document holds 1 to 128 tokens and one holds exactly 128.
All inputs are finite; a program needn't handle non-finite values.
Results may differ from a plain program's by a relative error of at most 0.02.
Values may be sent and summed in bfloat16 or wider, within the bound.
A program may use at most 640 MiB of HBM per device.

v0:
```python
import math

import jax
import jax.numpy as jnp
from jax import lax
from jax.sharding import PartitionSpec as P

HEAD_DIM = 64


EPS = 1e-05
THETA = 130000.0
SCALE = 0.125


def times_plain(left_op, right_op):
    return jnp.dot(left_op, right_op, preferred_element_type=jnp.float32)


def times_transposed(left_op, right_op):
    return lax.dot_general(
        left_op, right_op, (((1,), (1,)), ((), ())), preferred_element_type=jnp.float32
    )


def token_contract(left_op, right_op):
    return lax.dot_general(
        left_op, right_op, (((0,), (0,)), ((), ())), preferred_element_type=jnp.float32
    )


def positions_tables(segment_row, head_dim):
    length_all = segment_row.shape[0]
    counter = lax.iota(jnp.int32, length_all)
    is_first = jnp.concatenate([jnp.ones((1,), jnp.bool_), segment_row[1:] != segment_row[:-1]])
    first_at = lax.cummax(jnp.where(is_first, counter, jnp.zeros_like(counter)), axis=0)
    position = (counter - first_at).astype(jnp.float32)
    half_dim = head_dim // 2
    inverse = jnp.exp(
        -(jnp.arange(half_dim, dtype=jnp.float32) * (2.0 / head_dim)) * math.log(THETA)
    )
    angles = position[:, None] * inverse[None, :]
    return (jnp.cos(angles), jnp.sin(angles))


def rotate(values, cosine, sine_tab, direction, head_dim):
    row_count, total_width = values.shape
    half_dim = head_dim // 2
    halves = values.reshape(row_count, total_width // head_dim, 2, half_dim)
    first_half = halves[:, :, 0]
    second_half = halves[:, :, 1]
    cos_wide = cosine[:, None, :]
    sin_wide = direction * sine_tab[:, None, :]
    turned = jnp.stack(
        [
            first_half * cos_wide - second_half * sin_wide,
            second_half * cos_wide + first_half * sin_wide,
        ],
        axis=2,
    )
    return turned.reshape(row_count, total_width)


def allowed(segment_row, row_start, span_rows):
    length_all = segment_row.shape[0]
    row_ids = row_start + jnp.arange(span_rows, dtype=jnp.int32)
    col_ids = jnp.arange(length_all, dtype=jnp.int32)
    return (segment_row[:, None] == segment_row[None, :]) & (col_ids[None, :] <= row_ids[:, None])


def attention_forward(q_rot, k_rot, v_vals, segment_row, head_dim):
    row_count, total_width = q_rot.shape
    n_heads = total_width // head_dim
    span_rows = min(512, row_count)
    q_heads = q_rot.reshape(row_count, n_heads, head_dim)
    k_heads = k_rot.reshape(row_count, n_heads, head_dim)
    v_heads = v_vals.reshape(row_count, n_heads, head_dim)

    def one_block(block_id):
        row_start = block_id * span_rows
        scores = (
            jnp.einsum("qhd,khd->hqk", q_heads, k_heads, preferred_element_type=jnp.float32) * SCALE
        )
        scores = jnp.where(allowed(segment_row, row_start, span_rows)[None], scores, -1e30)
        log_total = jnp.log(jnp.sum(jnp.exp(scores), axis=-1))
        rounded_probs = jnp.exp(scores - log_total[..., None]).astype(jnp.bfloat16)
        mixed_out = jnp.einsum(
            "hqk,khd->qhd", rounded_probs, v_heads, preferred_element_type=jnp.float32
        )
        return (mixed_out.astype(jnp.bfloat16).reshape(span_rows, total_width), log_total)

    outputs, log_totals = lax.map(one_block, jnp.arange(row_count // span_rows, dtype=jnp.int32))
    return (
        outputs.reshape(row_count, total_width),
        log_totals.transpose(1, 0, 2).reshape(n_heads, row_count),
    )


def attention_backward(q_rot, k_rot, v_vals, log_totals, grad_att, segment_row, head_dim):
    row_count, total_width = q_rot.shape
    n_heads = total_width // head_dim
    span_rows = min(512, row_count)
    q_heads = q_rot.reshape(row_count, n_heads, head_dim)
    k_heads = k_rot.reshape(row_count, n_heads, head_dim)
    v_heads = v_vals.reshape(row_count, n_heads, head_dim)
    g_heads = grad_att.reshape(row_count, n_heads, head_dim)

    def one_block(carried, block_id):
        key_acc, value_acc = carried
        row_start = block_id * span_rows
        scores = (
            jnp.einsum("qhd,khd->hqk", q_heads, k_heads, preferred_element_type=jnp.float32) * SCALE
        )
        scores = jnp.where(allowed(segment_row, row_start, span_rows)[None], scores, -1e30)
        attn_probs = jnp.exp(scores - log_totals[..., None])
        grad_probs = jnp.einsum(
            "qhd,khd->hqk", g_heads, v_heads, preferred_element_type=jnp.float32
        )
        inner_sum = jnp.sum(attn_probs * grad_probs, axis=-1, keepdims=True)
        grad_scores = (attn_probs * (grad_probs - inner_sum) * SCALE).astype(jnp.bfloat16)
        rounded_probs = attn_probs.astype(jnp.bfloat16)
        grad_query = jnp.einsum(
            "hqk,khd->qhd", grad_scores, k_heads, preferred_element_type=jnp.float32
        )
        key_acc = key_acc + jnp.einsum(
            "hqk,qhd->khd", grad_scores, q_heads, preferred_element_type=jnp.float32
        )
        value_acc = value_acc + jnp.einsum(
            "hqk,qhd->khd", rounded_probs, g_heads, preferred_element_type=jnp.float32
        )
        return ((key_acc, value_acc), grad_query.reshape(span_rows, total_width))

    zeros_heads = jnp.zeros((row_count, n_heads, head_dim), jnp.float32)
    (key_acc, value_acc), grad_blocks = lax.scan(
        one_block, (zeros_heads, zeros_heads), jnp.arange(row_count // span_rows, dtype=jnp.int32)
    )
    return (
        grad_blocks.reshape(row_count, total_width),
        key_acc.reshape(row_count, total_width),
        value_acc.reshape(row_count, total_width),
    )


def normed_fold(source, scale_rows, pieces):
    gain_piece = pieces[-1]
    normed = (source * scale_rows * gain_piece.astype(jnp.float32)[None, :]).astype(jnp.bfloat16)
    running_sums = tuple((times_plain(normed, weight_piece) for weight_piece in pieces[:-1]))
    return running_sums + (normed, gain_piece)


def plain_fold(source, pieces):
    return times_plain(source, pieces[0])


def columns_fold(cotangents, pieces):
    column_part = times_transposed(cotangents[0], pieces[0])
    for cotan_now, weight_piece in zip(cotangents[1:], pieces[1:]):
        column_part = column_part + times_transposed(cotan_now, weight_piece)
    return column_part


def weight_grad(left_op, right_op):
    return lax.psum_scatter(
        token_contract(left_op, right_op).astype(jnp.bfloat16),
        "shard",
        scatter_dimension=0,
        tiled=True,
    ).astype(jnp.float32)


def per_device(
    block_input,
    segment_ids,
    attn_gain,
    mlp_gain,
    w_query,
    w_key,
    w_value,
    w_out,
    w_gate,
    w_up,
    w_down,
    out_grad,
):
    row_count, model_width = block_input.shape
    segment_row = segment_ids[0]
    cosine, sine_tab = positions_tables(segment_row, HEAD_DIM)
    input_f = block_input.astype(jnp.float32)
    scale_one = lax.rsqrt(jnp.mean(input_f * input_f, axis=-1, keepdims=True) + EPS)
    query_proj, key_proj, value_proj, normed_one, gain_one = normed_fold(
        input_f,
        scale_one,
        (
            lax.all_gather(w_query, "shard", axis=0, tiled=True),
            lax.all_gather(w_key, "shard", axis=0, tiled=True),
            lax.all_gather(w_value, "shard", axis=0, tiled=True),
            lax.all_gather(attn_gain, "shard", axis=0, tiled=True),
        ),
    )
    q_rot = rotate(query_proj, cosine, sine_tab, 1.0, HEAD_DIM).astype(jnp.bfloat16)
    k_rot = rotate(key_proj, cosine, sine_tab, 1.0, HEAD_DIM).astype(jnp.bfloat16)
    v_vals = value_proj.astype(jnp.bfloat16)
    attended, log_totals = attention_forward(q_rot, k_rot, v_vals, segment_row, HEAD_DIM)
    attn_proj = plain_fold(attended, (lax.all_gather(w_out, "shard", axis=0, tiled=True),))
    residual = input_f + attn_proj
    scale_two = lax.rsqrt(jnp.mean(residual * residual, axis=-1, keepdims=True) + EPS)
    gate_pre, up_pre, normed_two, gain_two = normed_fold(
        residual,
        scale_two,
        (
            lax.all_gather(w_gate, "shard", axis=0, tiled=True),
            lax.all_gather(w_up, "shard", axis=0, tiled=True),
            lax.all_gather(mlp_gain, "shard", axis=0, tiled=True),
        ),
    )
    gate_sig = jax.nn.sigmoid(gate_pre)
    silu_val = gate_pre * gate_sig
    hidden_b = (silu_val * up_pre).astype(jnp.bfloat16)
    ffn_proj = plain_fold(hidden_b, (lax.all_gather(w_down, "shard", axis=0, tiled=True),))
    block_output = (residual + ffn_proj).astype(jnp.bfloat16)
    grad_out_f = out_grad.astype(jnp.float32)
    grad_hidden = columns_fold((out_grad,), (lax.all_gather(w_down, "shard", axis=0, tiled=True),))
    down_term = weight_grad(hidden_b, out_grad)
    gate_b = (grad_hidden * up_pre * gate_sig * (1.0 + gate_pre * (1.0 - gate_sig))).astype(
        jnp.bfloat16
    )
    up_b = (grad_hidden * silu_val).astype(jnp.bfloat16)
    gate_term = weight_grad(normed_two, gate_b)
    up_term = weight_grad(normed_two, up_b)
    grad_normed_two = columns_fold(
        (gate_b, up_b),
        (
            lax.all_gather(w_gate, "shard", axis=0, tiled=True),
            lax.all_gather(w_up, "shard", axis=0, tiled=True),
        ),
    )
    gain_two_term = jnp.sum(grad_normed_two * residual * scale_two, axis=0)
    weighted_two = gain_two.astype(jnp.float32) * grad_normed_two
    grad_residual = (
        grad_out_f
        + scale_two * weighted_two
        - residual
        * (scale_two * scale_two * scale_two)
        * jnp.mean(weighted_two * residual, axis=-1, keepdims=True)
    )
    residual_b = grad_residual.astype(jnp.bfloat16)
    out_term = weight_grad(attended, residual_b)
    grad_att_f = columns_fold((residual_b,), (lax.all_gather(w_out, "shard", axis=0, tiled=True),))
    grad_att = grad_att_f.astype(jnp.bfloat16)
    grad_q, grad_k, grad_v = attention_backward(
        q_rot, k_rot, v_vals, log_totals, grad_att, segment_row, HEAD_DIM
    )
    q_back = rotate(grad_q, cosine, sine_tab, -1.0, HEAD_DIM).astype(jnp.bfloat16)
    k_back = rotate(grad_k, cosine, sine_tab, -1.0, HEAD_DIM).astype(jnp.bfloat16)
    v_back = grad_v.astype(jnp.bfloat16)
    query_term = weight_grad(normed_one, q_back)
    key_term = weight_grad(normed_one, k_back)
    value_term = weight_grad(normed_one, v_back)
    grad_normed_one = columns_fold(
        (q_back, k_back, v_back),
        (
            lax.all_gather(w_query, "shard", axis=0, tiled=True),
            lax.all_gather(w_key, "shard", axis=0, tiled=True),
            lax.all_gather(w_value, "shard", axis=0, tiled=True),
        ),
    )
    gain_one_term = jnp.sum(grad_normed_one * input_f * scale_one, axis=0)
    weighted_one = gain_one.astype(jnp.float32) * grad_normed_one
    input_grad = (
        grad_residual
        + scale_one * weighted_one
        - input_f
        * (scale_one * scale_one * scale_one)
        * jnp.mean(weighted_one * input_f, axis=-1, keepdims=True)
    )
    gains_total = lax.psum((gain_one_term, gain_two_term), ("replica", "shard"))
    piece_width = model_width // lax.axis_size("shard")
    offset_at = lax.axis_index("shard") * piece_width
    grad_attn_gain = lax.dynamic_slice_in_dim(gains_total[0], offset_at, piece_width)
    grad_mlp_gain = lax.dynamic_slice_in_dim(gains_total[1], offset_at, piece_width)
    summed = (
        lax.psum(query_term.astype(jnp.bfloat16), "replica").astype(jnp.float32),
        lax.psum(key_term.astype(jnp.bfloat16), "replica").astype(jnp.float32),
        lax.psum(value_term.astype(jnp.bfloat16), "replica").astype(jnp.float32),
        lax.psum(out_term.astype(jnp.bfloat16), "replica").astype(jnp.float32),
        lax.psum(gate_term.astype(jnp.bfloat16), "replica").astype(jnp.float32),
        lax.psum(up_term.astype(jnp.bfloat16), "replica").astype(jnp.float32),
        lax.psum(down_term.astype(jnp.bfloat16), "replica").astype(jnp.float32),
    )
    return (
        block_output,
        input_grad,
        summed[0],
        summed[1],
        summed[2],
        summed[3],
        summed[4],
        summed[5],
        summed[6],
        grad_attn_gain,
        grad_mlp_gain,
    )


def solution(mesh):
    placed = (
        P(("replica", "shard"), None),
        P(("replica", "shard"), None),
        P("shard"),
        P("shard"),
        P("shard", None),
        P("shard", None),
        P("shard", None),
        P("shard", None),
        P("shard", None),
        P("shard", None),
        P("shard", None),
        P(("replica", "shard"), None),
    )
    return jax.shard_map(
        per_device,
        mesh=mesh,
        in_specs=placed,
        out_specs=(
            P(("replica", "shard"), None),
            P(("replica", "shard"), None),
            P("shard", None),
            P("shard", None),
            P("shard", None),
            P("shard", None),
            P("shard", None),
            P("shard", None),
            P("shard", None),
            P("shard"),
            P("shard"),
        ),
        check_vma=False,
    )
```

profile of v0, /device:TPU:0, one launch (start us, length us, event | category | flops | bytes accessed | tf_op | source)
XLA Modules:
  0.0 5086.2 jit_solution(397663264740797070)
XLA Ops:
  12.0 22.8 all-gather
  35.4 17.3 all-gather.1
  54.6 82.8 %all-gather.10.cloned.1.call-done = bf16[2048,2048]{1,0:T(8,128)(2,1)} async-done(((bf16[256,2048]{1,0:T(8,128)(2,1)}), bf16[2048,2048]{1,0:T(8,128)(2,1)}) %all-gather.10.cloned.1.call-update) | async-done | bytes 8388624 | tf_op jit(solution)/shard_map/all_gather | solution.py:196
  144.1 118.2 %all-gather.14.cloned.1.call-done = bf16[2048,2048]{1,0:T(8,128)(2,1)} async-done(((bf16[256,2048]{1,0:T(8,128)(2,1)}), bf16[2048,2048]{1,0:T(8,128)(2,1)}) %all-gather.14.cloned.1.call-update) | async-done | bytes 8388624 | tf_op jit(solution)/shard_map/all_gather | solution.py:195
  262.3 8.2 fusion.54
  270.4 116.7 %all-gather.12.cloned.1.call-done = bf16[2048,2048]{1,0:T(8,128)(2,1)} async-done(((bf16[256,2048]{1,0:T(8,128)(2,1)}), bf16[2048,2048]{1,0:T(8,128)(2,1)}) %all-gather.12.cloned.1.call-update) | async-done | bytes 8388624 | tf_op jit(solution)/shard_map/all_gather | solution.py:194
  396.0 10.2 fusion.2
  411.4 100.3 %all-gather.16.cloned.1.call-done = bf16[2048,2048]{1,0:T(8,128)(2,1)} async-done(((bf16[256,2048]{1,0:T(8,128)(2,1)}), bf16[2048,2048]{1,0:T(8,128)(2,1)}) %all-gather.16.cloned.1.call-update) | async-done | bytes 8388624 | tf_op jit(solution)/shard_map/all_gather | solution.py:204
  519.4 629.6 %all-gather.18.cloned.1.call-done = bf16[2048,8192]{1,0:T(8,128)(2,1)} async-done(((bf16[256,8192]{1,0:T(8,128)(2,1)}), bf16[2048,8192]{1,0:T(8,128)(2,1)}) %all-gather.18.cloned.1.call-update) | async-done | bytes 33554448 | tf_op jit(solution)/shard_map/all_gather | solution.py:211
  1149.0 19.3 fusion.59
  1168.3 619.8 %all-gather.20.cloned.1.call-done = bf16[2048,8192]{1,0:T(8,128)(2,1)} async-done(((bf16[256,8192]{1,0:T(8,128)(2,1)}), bf16[2048,8192]{1,0:T(8,128)(2,1)}) %all-gather.20.cloned.1.call-update) | async-done | bytes 33554448 | tf_op jit(solution)/shard_map/all_gather | solution.py:212
  1788.1 19.1 fusion.60
  1807.2 620.1 %all-gather.22.cloned.1.call-done = bf16[8192,2048]{1,0:T(8,128)(2,1)} async-done(((bf16[1024,2048]{1,0:T(8,128)(2,1)}), bf16[8192,2048]{1,0:T(8,128)(2,1)}) %all-gather.22.cloned.1.call-update) | async-done | bytes 33554448 | tf_op jit(solution)/shard_map/all_gather | solution.py:219
  2427.3 24.0 multiply_convert_fusion.1
  2451.2 16.9 fusion.61
  2468.1 18.8 multiply_reduce_fusion.1
  2501.8 14.1 fusion.13
  2515.9 14.1 fusion.16
  2568.7 16.9 convolution_convert_fusion.2
  2585.9 16.6 convolution_convert_fusion.1
  2602.5 16.6 convolution_convert_fusion
  2619.4 69.1 %reduce-scatter.8.cloned.1.call-done = bf16[256,2048]{1,0:T(8,128)(2,1)} async-done(((bf16[2048,2048]{1,0:T(8,128)(2,1)}), bf16[256,2048]{1,0:T(8,128)(2,1)}) %reduce-scatter.8.cloned.1.call-update) | async-done | bytes 1048592 | tf_op jit(solution)/shard_map/reduce_scatter | solution.py:163
  2688.5 150.8 %reduce-scatter.10.cloned.1.call-done = bf16[256,2048]{1,0:T(8,128)(2,1)} async-done(((bf16[2048,2048]{1,0:T(8,128)(2,1)}), bf16[256,2048]{1,0:T(8,128)(2,1)}) %reduce-scatter.10.cloned.1.call-update) | async-done | bytes 1048592 | tf_op jit(solution)/shard_map/reduce_scatter | solution.py:163
  2839.3 150.7 %reduce-scatter.12.cloned.1.call-done = bf16[256,2048]{1,0:T(8,128)(2,1)} async-done(((bf16[2048,2048]{1,0:T(8,128)(2,1)}), bf16[256,2048]{1,0:T(8,128)(2,1)}) %reduce-scatter.12.cloned.1.call-update) | async-done | bytes 1048592 | tf_op jit(solution)/shard_map/reduce_scatter | solution.py:163
  2990.0 150.3 %reduce-scatter.14.cloned.1.call-done = bf16[256,2048]{1,0:T(8,128)(2,1)} async-done(((bf16[2048,2048]{1,0:T(8,128)(2,1)}), bf16[256,2048]{1,0:T(8,128)(2,1)}) %reduce-scatter.14.cloned.1.call-update) | async-done | bytes 1048592 | tf_op jit(solution)/shard_map/reduce_scatter | solution.py:163
  3140.3 541.9 %reduce-scatter.16.cloned.1.call-done = bf16[256,8192]{1,0:T(8,128)(2,1)} async-done(((bf16[2048,8192]{1,0:T(8,128)(2,1)}), bf16[256,8192]{1,0:T(8,128)(2,1)}) %reduce-scatter.16.cloned.1.call-update) | async-done | bytes 4194320 | tf_op jit(solution)/shard_map/reduce_scatter | solution.py:163
  3682.1 541.7 %reduce-scatter.18.cloned.1.call-done = bf16[256,8192]{1,0:T(8,128)(2,1)} async-done(((bf16[2048,8192]{1,0:T(8,128)(2,1)}), bf16[256,8192]{1,0:T(8,128)(2,1)}) %reduce-scatter.18.cloned.1.call-update) | async-done | bytes 4194320 | tf_op jit(solution)/shard_map/reduce_scatter | solution.py:163
  4223.8 541.4 %reduce-scatter.20.cloned.1.call-done = bf16[1024,2048]{1,0:T(8,128)(2,1)} async-done(((bf16[8192,2048]{1,0:T(8,128)(2,1)}), bf16[1024,2048]{1,0:T(8,128)(2,1)}) %reduce-scatter.20.cloned.1.call-update) | async-done | bytes 4194320 | tf_op jit(solution)/shard_map/reduce_scatter | solution.py:163
  4771.5 7.0 convolution_add_fusion.3
  4782.8 40.7 all-reduce
  4828.8 16.8 fusion.19
  4845.6 211.6 %all-reduce.4.cloned.1.call-done = (bf16[256,2048]{1,0:T(8,128)(2,1)}, bf16[256,2048]{1,0:T(8,128)(2,1)}, bf16[256,2048]{1,0:T(8,128)(2,1)}, bf16[256,2048]{1,0:...) async-done(((bf16[256,2048]{1,0:T(8,128)(2,1)}, bf16[256,2048]{1,0:T(8,128)(2,1)}, bf16[256,2048]{1,0:T(8,128)(2,1)}, ...) | async-done | bytes 16777232 | tf_op jit(solution)/shard_map/psum | solution.py:282
  (137 shorter events, 127.6 us)
Async XLA Ops:
  7.2 130.3 %all-gather.10.cloned.1.call-start = ((), (), s32[]{:S(2)}) async-start(), calls=%async_computation.7 | async-start | bytes 9437184 | tf_op jit(solution)/shard_map/all_gather | solution.py:196
  7.9 254.4 %all-gather.14.cloned.1.call-start = ((), (), s32[]{:S(2)}) async-start(), calls=%async_computation.9 | async-start | bytes 9437184 | tf_op jit(solution)/shard_map/all_gather | solution.py:195
  8.7 378.4 %all-gather.12.cloned.1.call-start = ((), (), s32[]{:S(2)}) async-start(), calls=%async_computation.8 | async-start | bytes 9437184 | tf_op jit(solution)/shard_map/all_gather | solution.py:194
  9.4 502.4 %all-gather.16.cloned.1.call-start = ((), (), s32[]{:S(2)}) async-start(), calls=%async_computation.10 | async-start | bytes 9437184 | tf_op jit(solution)/shard_map/all_gather | solution.py:204
  10.0 1139.1 %all-gather.18.cloned.1.call-start = ((), (), s32[]{:S(2)}) async-start(), calls=%async_computation.11 | async-start | bytes 37748736 | tf_op jit(solution)/shard_map/all_gather | solution.py:211
  10.6 24.2 copy-start.19
  10.6 24.8 copy-start.22
  10.6 42.2 copy-start
  10.6 1777.5 %all-gather.20.cloned.1.call-start = ((), (), s32[]{:S(2)}) async-start(), calls=%async_computation.12 | async-start | bytes 37748736 | tf_op jit(solution)/shard_map/all_gather | solution.py:212
  11.2 2416.1 %all-gather.22.cloned.1.call-start = ((), (), s32[]{:S(2)}) async-start(), calls=%async_computation.13 | async-start | bytes 37748736 | tf_op jit(solution)/shard_map/all_gather | solution.py:219
  11.9 2676.6 %reduce-scatter.8.cloned.1.call-start = ((), (), s32[]{:S(2)}) async-start(), calls=%async_computation.14 | async-start | bytes 9437184 | tf_op jit(solution)/shard_map/reduce_scatter | solution.py:163
  144.1 262.2 %copy-start.3 = (bf16[256,2048]{0,1:T(8,128)(2,1)}, bf16[256,2048]{0,1:T(8,128)(2,1)S(1)}, u32[]{:S(2)}) copy-start(bf16[256,2048]{0,1:T(8,128)(2,1)S(1)} %copy.45) | copy-start | bytes 3145732
  387.1 7.0 copy-start.14
  396.0 10.2 copy-start.17
  517.9 1950.2 %copy-start.1 = (f32[256,2048]{1,0:T(8,128)}, f32[256,2048]{1,0:T(8,128)S(1)}, u32[]{:S(2)}) copy-start(f32[256,2048]{1,0:T(8,128)S(1)} %get-tuple-element.98) | copy-start | bytes 6291460
  2468.1 21.6 slice-start
  2468.1 18.8 copy-start.8
  2468.1 21.6 slice-start.1
  2515.9 14.1 copy-start.18
  2541.0 298.4 %reduce-scatter.10.cloned.1.call-start = ((), (), s32[]{:S(2)}) async-start(), calls=%async_computation.15 | async-start | bytes 9437184 | tf_op jit(solution)/shard_map/reduce_scatter | solution.py:163
  2549.3 440.6 %reduce-scatter.12.cloned.1.call-start = ((), (), s32[]{:S(2)}) async-start(), calls=%async_computation.16 | async-start | bytes 9437184 | tf_op jit(solution)/shard_map/reduce_scatter | solution.py:163
  2561.8 578.5 %reduce-scatter.14.cloned.1.call-start = ((), (), s32[]{:S(2)}) async-start(), calls=%async_computation.17 | async-start | bytes 9437184 | tf_op jit(solution)/shard_map/reduce_scatter | solution.py:163
  2568.7 1113.4 %reduce-scatter.16.cloned.1.call-start = ((), (), s32[]{:S(2)}) async-start(), calls=%async_computation.18 | async-start | bytes 37748736 | tf_op jit(solution)/shard_map/reduce_scatter | solution.py:163
  2585.6 1638.2 %reduce-scatter.18.cloned.1.call-start = ((), (), s32[]{:S(2)}) async-start(), calls=%async_computation.19 | async-start | bytes 37748736 | tf_op jit(solution)/shard_map/reduce_scatter | solution.py:163
  2602.5 2162.7 %reduce-scatter.20.cloned.1.call-start = ((), (), s32[]{:S(2)}) async-start(), calls=%async_computation.20 | async-start | bytes 37748736 | tf_op jit(solution)/shard_map/reduce_scatter | solution.py:163
  2619.1 2438.0 %all-reduce.4.cloned.1.call-start = ((), (), s32[]{:S(2)}) async-start(), calls=%async_computation.21 | async-start | bytes 33554432 | tf_op jit(solution)/shard_map/psum | solution.py:282
  4765.2 6.3 copy-start.13
  4765.2 13.3 slice-start.2
  4771.5 7.1 copy-start.10
  4771.5 7.1 slice-start.3
  4778.6 46.2 copy-start.20
  5057.2 7.4 copy-start.15
  (10 other events, 35.8 us)
Sparse Core Ops, SparseCore 0:
  10.1 127.3 all-gather.9
  139.6 122.6 all-gather.13
  264.4 122.6 all-gather.11
  389.1 122.6 all-gather.15
  513.1 635.8 all-gather.17
  1150.4 637.6 all-gather.19
  1789.6 637.6 all-gather.21
  2541.1 147.3 reduce-scatter.7
  2692.7 146.5 reduce-scatter.9
  2843.4 146.5 reduce-scatter.11
  2993.6 146.5 reduce-scatter.13
  3143.9 538.1 reduce-scatter.15
  3685.9 537.8 reduce-scatter.17
  4227.4 537.7 reduce-scatter.19
  4768.3 288.8 all-reduce.3
where the time goes:
time: 5090 us
  waiting for transfers between devices  4650 us (91%)
  matrix products  292 us (6%)
  blocking collectives  80.8 us (2%)
    reduce_scatter x7, waiting for transfers between devices, weight_grad(): lax.psum_scatter(token_contract(left_op, right_op).astype(jnp.bfloat16),...  2150 us
    all_gather x1, waiting for transfers between devices, per_device(): lax.all_gather(w_gate, 'shard', axis=0, tiled=True)  630 us
    all_gather x1, waiting for transfers between devices, per_device(): lax.all_gather(w_down, 'shard', axis=0, tiled=True)  620 us
    all_gather x1, waiting for transfers between devices, per_device(): lax.all_gather(w_up, 'shard', axis=0, tiled=True)  620 us
    psum x1, waiting for transfers between devices, per_device(): lax.psum(query_term.astype(jnp.bfloat16), 'replica').astype(jnp.float32)  212 us
    all_gather x1, waiting for transfers between devices, per_device(): lax.all_gather(w_key, 'shard', axis=0, tiled=True)  118 us
    all_gather x1, waiting for transfers between devices, per_device(): lax.all_gather(w_query, 'shard', axis=0, tiled=True)  117 us
  transfers between devices with their start and end apart: 15, of which 15 were waited for; matrix products, arithmetic and copies ran while one was open for 4% of the time, Pallas kernels for 0%

commit v1 on v0

v1 whole, which is shorter than its diff:
```python
import functools
import math

import jax
import jax.numpy as jnp
from jax import lax
from jax.experimental import pallas as pl
from jax.experimental.pallas import tpu as pltpu
from jax.sharding import PartitionSpec as P

MESH = pl.DeviceIdType.MESH

HEAD_DIM = 64


EPS = 1e-05
THETA = 130000.0
SCALE = 0.125


def times_plain(left_op, right_op):
    return jnp.dot(left_op, right_op, preferred_element_type=jnp.float32)


def times_transposed(left_op, right_op):
    return lax.dot_general(
        left_op, right_op, (((1,), (1,)), ((), ())), preferred_element_type=jnp.float32
    )


def token_contract(left_op, right_op):
    return lax.dot_general(
        left_op, right_op, (((0,), (0,)), ((), ())), preferred_element_type=jnp.float32
    )


def split_rows(rows):
    unit = 16
    across = (rows // unit) * 3 // 16 * unit
    rest = (rows - across) // unit
    count = min(4, rest)
    sizes = [(rest // count + (1 if i >= count - rest % count else 0)) * unit for i in range(count)]
    chunks, at = [], across
    for size in sizes:
        chunks.append((at, size))
        at += size
    return across, chunks


def use_kernels(n, rows):
    return n % 2 == 0 and 2 < n <= 8 and rows % 256 == 0


def wire_cost(size):
    return pl.CostEstimate(flops=0, bytes_accessed=30 * size, transcendentals=0)


class Copies:
    def __init__(self):
        self.started = []

    def start(self, cond, src, dst, send_sem, recv_sem, target, axis="shard"):
        copy = pltpu.make_async_remote_copy(
            src_ref=src,
            dst_ref=dst,
            send_sem=send_sem,
            recv_sem=recv_sem,
            device_id={axis: target},
            device_id_type=MESH,
        )
        if cond is None:
            copy.start()
        else:
            pl.when(cond)(copy.start)
        self.started.append((cond, copy))

    def finish(self):
        for cond, copy in self.started:
            if cond is None:
                copy.wait_send()
            else:
                pl.when(cond)(copy.wait_send)


def wait_arrival(dst, send_sem, recv_sem, source, axis="shard"):
    pltpu.make_async_remote_copy(
        src_ref=dst,
        dst_ref=dst,
        send_sem=send_sem,
        recv_sem=recv_sem,
        device_id={axis: source},
        device_id_type=MESH,
    ).wait_recv()


def greet(has_left, has_right, left, right, other):
    barrier = pltpu.get_barrier_semaphore()
    pl.semaphore_signal(barrier, inc=1, device_id={"shard": other}, device_id_type=MESH)

    @pl.when(has_left)
    def _():
        pl.semaphore_signal(barrier, inc=1, device_id={"shard": left}, device_id_type=MESH)

    @pl.when(has_right)
    def _():
        pl.semaphore_signal(barrier, inc=1, device_id={"shard": right}, device_id_type=MESH)

    pl.semaphore_wait(barrier, 1 + has_left.astype(jnp.int32) + has_right.astype(jnp.int32))


def gather_kernel(n, across, chunks, x_ref, o_ref, own_sem, z_send, z_recv, y_send, y_recv):
    length = n // 2
    count = len(chunks)
    me = lax.axis_index("shard")
    place, side = me // 2, me % 2
    other = me + 1 - 2 * side
    has_left, has_right = place > 0, place < length - 1
    nexts = ((has_right, me + 2), (has_left, me - 2))
    greet(has_left, has_right, me - 2, me + 2, other)
    copies = Copies()
    own = pltpu.make_async_copy(x_ref, o_ref.at[me], own_sem)
    own.start()
    first = pl.ds(0, across)
    y_first = (2 * length - 1) * count
    copies.start(
        None, x_ref.at[first], o_ref.at[me, first], y_send.at[y_first], y_recv.at[y_first], other
    )

    def z_hop(direction, hop, slot, src, dst):
        cond, target = nexts[direction]
        copies.start(
            cond,
            src,
            dst,
            z_send.at[direction, hop, slot],
            z_recv.at[direction, hop, slot],
            target,
        )

    def y_hop(origin, chunk, src, dst, cond, key):
        copies.start(cond, src, dst, y_send.at[key], y_recv.at[key], other)

    for c, (at, size) in enumerate(chunks):
        span = pl.ds(at, size)
        for direction in range(2):
            z_hop(direction, 0, c, x_ref.at[span], o_ref.at[me, span])
        y_hop(me, c, x_ref.at[span], o_ref.at[me, span], None, c)
    for hop in range(1, length):
        for c, (at, size) in enumerate(chunks):
            span = pl.ds(at, size)
            for direction in range(2):
                source = me - 2 * hop if direction == 0 else me + 2 * hop
                exists = source >= 0 if direction == 0 else source < n
                sender = me - 2 if direction == 0 else me + 2

                @pl.when(exists)
                def _():
                    wait_arrival(
                        o_ref.at[source, span],
                        z_send.at[direction, hop - 1, c],
                        z_recv.at[direction, hop - 1, c],
                        sender,
                    )

                here = o_ref.at[source, span]
                if hop < length - 1:
                    cond, target = nexts[direction]
                    copies.start(
                        jnp.logical_and(exists, cond),
                        here,
                        here,
                        z_send.at[direction, hop, c],
                        z_recv.at[direction, hop, c],
                        target,
                    )
                key = (1 + direction * (length - 1) + hop - 1) * count + c
                copies.start(exists, here, here, y_send.at[key], y_recv.at[key], other)
    wait_arrival(o_ref.at[other, first], y_send.at[y_first], y_recv.at[y_first], other)
    for direction in range(2):
        z_hop(direction, 0, count, x_ref.at[first], o_ref.at[me, first])
        z_hop(direction, 0, count + 1, o_ref.at[other, first], o_ref.at[other, first])
    for hop in range(1, length):
        for line, base in enumerate((me, other)):
            for direction in range(2):
                source = base - 2 * hop if direction == 0 else base + 2 * hop
                exists = source >= 0 if direction == 0 else source < n
                sender = me - 2 if direction == 0 else me + 2

                @pl.when(exists)
                def _():
                    wait_arrival(
                        o_ref.at[source, first],
                        z_send.at[direction, hop - 1, count + line],
                        z_recv.at[direction, hop - 1, count + line],
                        sender,
                    )

                here = o_ref.at[source, first]
                if hop < length - 1:
                    cond, target = nexts[direction]
                    copies.start(
                        jnp.logical_and(exists, cond),
                        here,
                        here,
                        z_send.at[direction, hop, count + line],
                        z_recv.at[direction, hop, count + line],
                        target,
                    )
    for c, (at, size) in enumerate(chunks):
        span = pl.ds(at, size)
        wait_arrival(o_ref.at[other, span], y_send.at[c], y_recv.at[c], other)
        for hop in range(1, length):
            for direction in range(2):
                source = other - 2 * hop if direction == 0 else other + 2 * hop
                exists = source >= 0 if direction == 0 else source < n
                key = (1 + direction * (length - 1) + hop - 1) * count + c

                @pl.when(exists)
                def _():
                    wait_arrival(o_ref.at[source, span], y_send.at[key], y_recv.at[key], other)

    own.wait()
    copies.finish()


def gather_rows(x):
    n = lax.axis_size("shard")
    rows, columns = x.shape
    if not use_kernels(n, rows):
        return lax.all_gather(x, "shard", axis=0, tiled=False)
    across, chunks = split_rows(rows)
    length, count = n // 2, len(chunks)
    keys = (2 * length - 1) * count + 1
    return pl.pallas_call(
        functools.partial(gather_kernel, n, across, chunks),
        out_shape=jax.ShapeDtypeStruct((n, rows, columns), x.dtype),
        in_specs=[pl.BlockSpec(memory_space=pltpu.VMEM)],
        out_specs=pl.BlockSpec(memory_space=pl.ANY),
        scratch_shapes=[
            pltpu.SemaphoreType.DMA,
            pltpu.SemaphoreType.DMA((2, length - 1, count + 2)),
            pltpu.SemaphoreType.DMA((2, length - 1, count + 2)),
            pltpu.SemaphoreType.DMA((keys,)),
            pltpu.SemaphoreType.DMA((keys,)),
        ],
        compiler_params=pltpu.CompilerParams(collective_id=1, has_side_effects=True),
        cost_estimate=wire_cost(n * rows * columns * 2),
        name="gather_rows",
    )(x)


def add_rows(*terms):
    total = terms[0].astype(jnp.float32)
    for term in terms[1:]:
        total = total + term.astype(jnp.float32)
    return total


def scatter_kernel(
    n, across, chunks, p_ref, o_ref, y_buf, z_buf, a_buf, a_got, z_send, z_recv, y_send, y_recv
):
    length = n // 2
    count = len(chunks)
    me = lax.axis_index("shard")
    place, side = me // 2, me % 2
    other = me + 1 - 2 * side
    has_left, has_right = place > 0, place < length - 1
    greet(has_left, has_right, me - 2, me + 2, other)
    copies = Copies()
    first = pl.ds(0, across)

    def routes():
        for distance in range(length - 1, 0, -1):
            yield 0, distance, place + distance, place + distance < length
            yield 1, distance, place - distance, place - distance >= 0

    behind = (has_left, has_right)
    sender = (me - 2, me + 2)
    target = (me + 2, me - 2)

    for direction, distance, owner, exists in routes():
        for c, (at, size) in enumerate(chunks):
            key = (direction * (length - 1) + distance - 1) * count + c
            copies.start(
                exists,
                p_ref.at[2 * owner + 1 - side, pl.ds(at, size)],
                y_buf.at[direction * (length - 1) + distance - 1, pl.ds(at - across, size)],
                y_send.at[key],
                y_recv.at[key],
                other,
            )
    mid = 2 * (length - 1)
    for c, (at, size) in enumerate(chunks):
        key = mid * count + c
        copies.start(
            None,
            p_ref.at[2 * place + 1 - side, pl.ds(at, size)],
            y_buf.at[mid, pl.ds(at - across, size)],
            y_send.at[key],
            y_recv.at[key],
            other,
        )

    def z_dst(direction, distance, at, size):
        return z_buf.at[direction, distance, pl.ds(at, size)]

    for direction, distance, owner, exists in routes():
        for line in range(2):
            block = 2 * owner + (side if line == 0 else 1 - side)
            sem_in = (direction, distance, count + line)
            sem_out = (direction, distance - 1, count + line)
            place_rows = line * across
            from_start = jnp.logical_and(exists, jnp.logical_not(behind[direction]))
            passing = jnp.logical_and(exists, behind[direction])
            dst = z_dst(direction, distance - 1, place_rows, across)
            copies.start(
                from_start,
                p_ref.at[block, first],
                dst,
                z_send.at[sem_out],
                z_recv.at[sem_out],
                target[direction],
            )
            if distance < length - 1:
                here = z_dst(direction, distance, place_rows, across)

                @pl.when(passing)
                def _():
                    wait_arrival(here, z_send.at[sem_in], z_recv.at[sem_in], sender[direction])
                    here[...] = add_rows(here[...], p_ref[block, first]).astype(here.dtype)

                copies.start(
                    passing, here, dst, z_send.at[sem_out], z_recv.at[sem_out], target[direction]
                )

    for line in (1, 0):
        block = 2 * place + (side if line == 0 else 1 - side)
        o_ref[first] = p_ref[block, first].astype(jnp.float32)
        for direction in range(2):
            sem_in = (direction, 0, count + line)
            here = z_dst(direction, 0, line * across, across)

            @pl.when(behind[direction])
            def _():
                wait_arrival(here, z_send.at[sem_in], z_recv.at[sem_in], sender[direction])
                o_ref[first] = o_ref[first] + here[...].astype(jnp.float32)

        if line == 1:
            a_buf[...] = o_ref[first].astype(a_buf.dtype)
            key = (mid + 1) * count
            copies.start(None, a_buf, a_got, y_send.at[key], y_recv.at[key], other)

    for direction, distance, owner, exists in routes():
        slot = direction * (length - 1) + distance - 1
        for c, (at, size) in enumerate(chunks):
            key = slot * count + c
            held = y_buf.at[slot, pl.ds(at - across, size)]
            block = 2 * owner + side
            sem_in = (direction, distance, c)
            sem_out = (direction, distance - 1, c)
            rows_at = across + at
            span = pl.ds(at, size)

            @pl.when(exists)
            def _():
                wait_arrival(held, y_send.at[key], y_recv.at[key], other)

            if distance < length - 1:
                here = z_dst(direction, distance, rows_at, size)

                @pl.when(jnp.logical_and(exists, behind[direction]))
                def _():
                    wait_arrival(here, z_send.at[sem_in], z_recv.at[sem_in], sender[direction])
                    held[...] = add_rows(held[...], p_ref[block, span], here[...]).astype(
                        held.dtype
                    )

            @pl.when(jnp.logical_and(exists, jnp.logical_not(behind[direction])))
            def _():
                held[...] = add_rows(held[...], p_ref[block, span]).astype(held.dtype)

            copies.start(
                exists,
                held,
                z_dst(direction, distance - 1, rows_at, size),
                z_send.at[sem_out],
                z_recv.at[sem_out],
                target[direction],
            )
    for c, (at, size) in enumerate(chunks):
        key = mid * count + c
        held = y_buf.at[mid, pl.ds(at - across, size)]
        span = pl.ds(at, size)
        wait_arrival(held, y_send.at[key], y_recv.at[key], other)
        o_ref[span] = add_rows(held[...], p_ref[me, span])
        for direction in range(2):
            sem_in = (direction, 0, c)
            here = z_dst(direction, 0, across + at, size)

            @pl.when(behind[direction])
            def _():
                wait_arrival(here, z_send.at[sem_in], z_recv.at[sem_in], sender[direction])
                o_ref[span] = o_ref[span] + here[...].astype(jnp.float32)

    key = (mid + 1) * count
    wait_arrival(a_got, y_send.at[key], y_recv.at[key], other)
    o_ref[first] = o_ref[first] + a_got[...].astype(jnp.float32)
    copies.finish()


def scatter_rows(partial):
    n, rows, columns = partial.shape
    if not use_kernels(n, rows):
        return lax.psum_scatter(
            partial.reshape(n * rows, columns), "shard", scatter_dimension=0, tiled=True
        ).astype(jnp.float32)
    across, chunks = split_rows(rows)
    length, count = n // 2, len(chunks)
    late = rows - across
    keys = (2 * length - 1) * count + 1
    dtype = partial.dtype
    return pl.pallas_call(
        functools.partial(scatter_kernel, n, across, chunks),
        out_shape=jax.ShapeDtypeStruct((rows, columns), jnp.float32),
        in_specs=[pl.BlockSpec(memory_space=pltpu.VMEM)],
        out_specs=pl.BlockSpec(memory_space=pltpu.VMEM),
        scratch_shapes=[
            pltpu.VMEM((2 * length - 1, late, columns), dtype),
            pltpu.VMEM((2, length - 1, across + rows, columns), dtype),
            pltpu.VMEM((across, columns), dtype),
            pltpu.VMEM((across, columns), dtype),
            pltpu.SemaphoreType.DMA((2, length - 1, count + 2)),
            pltpu.SemaphoreType.DMA((2, length - 1, count + 2)),
            pltpu.SemaphoreType.DMA((keys,)),
            pltpu.SemaphoreType.DMA((keys,)),
        ],
        compiler_params=pltpu.CompilerParams(collective_id=2, has_side_effects=True),
        cost_estimate=wire_cost(n * rows * columns * 2),
        name="scatter_rows",
    )(partial)


def small_gather_kernel(n, a_ref, b_ref, a_out, b_out, send, recv):
    me = lax.axis_index("shard")
    barrier = pltpu.get_barrier_semaphore()
    peers = [lax.rem(me + d, n) for d in range(1, n)]
    for peer in peers:
        pl.semaphore_signal(barrier, inc=1, device_id={"shard": peer}, device_id_type=MESH)
    pl.semaphore_wait(barrier, n - 1)
    copies = Copies()
    for d, peer in enumerate(peers):
        for k, (src, dst) in enumerate(((a_ref, a_out), (b_ref, b_out))):
            copies.start(None, src, dst.at[me], send.at[k, d], recv.at[k, d], peer)
    a_out[me] = a_ref[...]
    b_out[me] = b_ref[...]
    for d in range(1, n):
        source = lax.rem(me + n - d, n)
        for k, dst in enumerate((a_out, b_out)):
            wait_arrival(dst.at[source], send.at[k, d - 1], recv.at[k, d - 1], source)
    copies.finish()


def gather_small(gains, segment_ids):
    n = lax.axis_size("shard")
    width, length = gains.shape[1], segment_ids.shape[1]
    if not use_kernels(n, 256) or width % 128 or length % 128:
        gains = lax.all_gather(gains, "shard", axis=1, tiled=True)
        return gains, lax.all_gather(segment_ids, "shard", axis=0, tiled=True)
    gains = jnp.pad(gains.astype(jnp.float32), ((0, 6), (0, 0)))
    ids = jnp.broadcast_to(segment_ids, (8, length))
    all_gains, all_ids = pl.pallas_call(
        functools.partial(small_gather_kernel, n),
        out_shape=(
            jax.ShapeDtypeStruct((n, 8, width), jnp.float32),
            jax.ShapeDtypeStruct((n, 8, length), jnp.int32),
        ),
        in_specs=[pl.BlockSpec(memory_space=pltpu.VMEM)] * 2,
        out_specs=[pl.BlockSpec(memory_space=pltpu.VMEM)] * 2,
        scratch_shapes=[pltpu.SemaphoreType.DMA((2, n - 1)), pltpu.SemaphoreType.DMA((2, n - 1))],
        compiler_params=pltpu.CompilerParams(collective_id=3, has_side_effects=True),
        name="gather_small",
    )(gains, ids)
    return all_gains[:, :2].transpose(1, 0, 2).reshape(2, n * width), all_ids[:, 0]


def small_sum_kernel(n, m, t_ref, o_ref, got, mine, shared, send, recv, send_two, recv_two):
    me, copy = lax.axis_index("shard"), lax.axis_index("replica")
    barrier = pltpu.get_barrier_semaphore()
    peers = [lax.rem(me + d, n) for d in range(1, n)]
    twins = [lax.rem(copy + d, m) for d in range(1, m)]
    for peer in peers:
        pl.semaphore_signal(barrier, inc=1, device_id={"shard": peer}, device_id_type=MESH)
    for twin in twins:
        pl.semaphore_signal(barrier, inc=1, device_id={"replica": twin}, device_id_type=MESH)
    pl.semaphore_wait(barrier, n + m - 2)
    copies = Copies()
    for d, peer in enumerate(peers):
        copies.start(None, t_ref.at[peer], got.at[me], send.at[d], recv.at[d], peer)
    got[me] = t_ref[me]
    for d in range(1, n):
        source = lax.rem(me + n - d, n)
        wait_arrival(got.at[source], send.at[d - 1], recv.at[d - 1], source)
    total = got[0]
    for i in range(1, n):
        total = total + got[i]
    mine[...] = total
    shared[copy] = total
    for d, twin in enumerate(twins):
        copies.start(
            None, mine, shared.at[copy], send_two.at[d], recv_two.at[d], twin, axis="replica"
        )
    for d in range(1, m):
        source = lax.rem(copy + m - d, m)
        wait_arrival(
            shared.at[source], send_two.at[d - 1], recv_two.at[d - 1], source, axis="replica"
        )
    total = shared[0]
    for i in range(1, m):
        total = total + shared[i]
    o_ref[...] = total
    copies.finish()


def sum_small(terms):
    n, m = lax.axis_size("shard"), lax.axis_size("replica")
    width = terms.shape[1] // n
    if not use_kernels(n, 256) or width % 128:
        total = lax.psum(terms, ("replica", "shard"))
        return lax.dynamic_slice_in_dim(total, lax.axis_index("shard") * width, width, axis=1)
    pieces = jnp.pad(terms, ((0, 6), (0, 0))).reshape(8, n, width).transpose(1, 0, 2)
    return pl.pallas_call(
        functools.partial(small_sum_kernel, n, m),
        out_shape=jax.ShapeDtypeStruct((8, width), jnp.float32),
        in_specs=[pl.BlockSpec(memory_space=pltpu.VMEM)],
        out_specs=pl.BlockSpec(memory_space=pltpu.VMEM),
        scratch_shapes=[
            pltpu.VMEM((n, 8, width), jnp.float32),
            pltpu.VMEM((8, width), jnp.float32),
            pltpu.VMEM((m, 8, width), jnp.float32),
            pltpu.SemaphoreType.DMA((n - 1,)),
            pltpu.SemaphoreType.DMA((n - 1,)),
            pltpu.SemaphoreType.DMA((m - 1,)),
            pltpu.SemaphoreType.DMA((m - 1,)),
        ],
        compiler_params=pltpu.CompilerParams(collective_id=4, has_side_effects=True),
        name="sum_small",
    )(pieces)[:2]


def after(x, *others):
    return lax.optimization_barrier((x,) + others)[0]


def to_columns(weights):
    n, copies = lax.axis_size("shard"), lax.axis_size("replica")
    me = lax.axis_index("replica")
    rows = weights[0].shape[0]
    part = rows // copies
    pieces = [
        lax.dynamic_slice_in_dim(w, me * part, part).reshape(part, n, -1).transpose(1, 0, 2)
        for w in weights
    ]
    swapped = lax.all_to_all(
        jnp.concatenate(pieces, axis=2), "shard", split_axis=0, concat_axis=0, tiled=True
    )
    shared = lax.all_gather(swapped, "replica", axis=1, tiled=False)
    return shared.reshape(n * rows, -1)


def sum_copies(grads):
    n, copies = lax.axis_size("shard"), lax.axis_size("replica")
    rows, width = grads.shape[0] // n, grads.shape[1]
    split = grads.reshape(n, copies, rows // copies, width).transpose(1, 0, 2, 3)
    return lax.psum_scatter(split, "replica", scatter_dimension=0, tiled=False)


def unpack_kernel(widths, x_ref, *o_refs):
    copies, _, part, _ = x_ref.shape
    at = 0
    for width, o_ref in zip(widths, o_refs):
        for r in range(copies):
            o_ref[pl.ds(r * part, part)] = x_ref[r, 0, :, pl.ds(at, width)].astype(o_ref.dtype)
        at += width


def to_rows(summed, widths):
    swapped = lax.all_to_all(summed, "shard", split_axis=0, concat_axis=0, tiled=True)
    return unpack(lax.all_gather(swapped, "replica", axis=0, tiled=False), widths)


def unpack(shared, widths):
    copies, n, part, total = shared.shape
    rows = copies * part
    if part % 16 == 0 and all(width % 128 == 0 for width in widths):
        return pl.pallas_call(
            functools.partial(unpack_kernel, widths),
            grid=(n,),
            out_shape=[jax.ShapeDtypeStruct((rows, n * width), jnp.float32) for width in widths],
            in_specs=[pl.BlockSpec((copies, 1, part, total), lambda i: (0, i, 0, 0))],
            out_specs=[pl.BlockSpec((rows, width), lambda i: (0, i)) for width in widths],
            name="unpack",
        )(shared)
    out, at = [], 0
    for width in widths:
        piece = shared[..., at : at + width].transpose(0, 2, 1, 3).reshape(rows, n * width)
        out.append(piece.astype(jnp.float32))
        at += width
    return out


def positions_tables(segment_rows, head_dim):
    length_all = segment_rows.shape[1]
    counter = lax.broadcasted_iota(jnp.int32, segment_rows.shape, 1)
    is_first = jnp.concatenate(
        [
            jnp.ones((segment_rows.shape[0], 1), jnp.bool_),
            segment_rows[:, 1:] != segment_rows[:, :-1],
        ],
        axis=1,
    )
    first_at = lax.cummax(jnp.where(is_first, counter, jnp.zeros_like(counter)), axis=1)
    position = (counter - first_at).astype(jnp.float32).reshape(-1)
    half_dim = head_dim // 2
    inverse = jnp.exp(
        -(jnp.arange(half_dim, dtype=jnp.float32) * (2.0 / head_dim)) * math.log(THETA)
    )
    angles = position[:, None] * inverse[None, :]
    return (jnp.cos(angles), jnp.sin(angles))


def rotate(values, cosine, sine_tab, direction, head_dim):
    row_count, total_width = values.shape
    half_dim = head_dim // 2
    halves = values.reshape(row_count, total_width // head_dim, 2, half_dim)
    first_half = halves[:, :, 0]
    second_half = halves[:, :, 1]
    cos_wide = cosine[:, None, :]
    sin_wide = direction * sine_tab[:, None, :]
    turned = jnp.stack(
        [
            first_half * cos_wide - second_half * sin_wide,
            second_half * cos_wide + first_half * sin_wide,
        ],
        axis=2,
    )
    return turned.reshape(row_count, total_width)


def allowed(segment_rows):
    ids = jnp.arange(segment_rows.shape[1], dtype=jnp.int32)
    return (segment_rows[:, :, None] == segment_rows[:, None, :]) & (
        ids[None, None, :] <= ids[None, :, None]
    )


def heads_of(values, packs, head_dim):
    return values.reshape(packs, values.shape[0] // packs, -1, head_dim)


def pair_scores(q_heads, k_heads, mask):
    scores = (
        jnp.einsum("pqhd,pkhd->phqk", q_heads, k_heads, preferred_element_type=jnp.float32) * SCALE
    )
    return jnp.where(mask[:, None], scores, -1e30)


def attention_forward(q_rot, k_rot, v_vals, segment_rows, head_dim):
    packs = segment_rows.shape[0]
    q_heads, k_heads, v_heads = (heads_of(v, packs, head_dim) for v in (q_rot, k_rot, v_vals))
    scores = pair_scores(q_heads, k_heads, allowed(segment_rows))
    log_total = jnp.log(jnp.sum(jnp.exp(scores), axis=-1))
    rounded_probs = jnp.exp(scores - log_total[..., None]).astype(jnp.bfloat16)
    mixed_out = jnp.einsum(
        "phqk,pkhd->pqhd", rounded_probs, v_heads, preferred_element_type=jnp.float32
    )
    return mixed_out.astype(jnp.bfloat16).reshape(q_rot.shape), log_total


def attention_backward(q_rot, k_rot, v_vals, log_total, grad_att, segment_rows, head_dim):
    packs = segment_rows.shape[0]
    q_heads, k_heads, v_heads, g_heads = (
        heads_of(v, packs, head_dim) for v in (q_rot, k_rot, v_vals, grad_att)
    )
    scores = pair_scores(q_heads, k_heads, allowed(segment_rows))
    attn_probs = jnp.exp(scores - log_total[..., None])
    grad_probs = jnp.einsum("pqhd,pkhd->phqk", g_heads, v_heads, preferred_element_type=jnp.float32)
    inner_sum = jnp.sum(attn_probs * grad_probs, axis=-1, keepdims=True)
    grad_scores = (attn_probs * (grad_probs - inner_sum) * SCALE).astype(jnp.bfloat16)
    rounded_probs = attn_probs.astype(jnp.bfloat16)
    grad_q = jnp.einsum("phqk,pkhd->pqhd", grad_scores, k_heads, preferred_element_type=jnp.float32)
    grad_k = jnp.einsum("phqk,pqhd->pkhd", grad_scores, q_heads, preferred_element_type=jnp.float32)
    grad_v = jnp.einsum(
        "phqk,pqhd->pkhd", rounded_probs, g_heads, preferred_element_type=jnp.float32
    )
    return tuple(g.reshape(q_rot.shape) for g in (grad_q, grad_k, grad_v))


def turn(values, cosine, sine_tab, direction):
    lane = lax.broadcasted_iota(jnp.int32, values.shape, 1)
    is_first = lane % HEAD_DIM < HEAD_DIM // 2
    width = values.shape[1]
    swapped = jnp.where(
        is_first,
        pltpu.roll(values, width - HEAD_DIM // 2, 1),
        pltpu.roll(values, HEAD_DIM // 2, 1),
    )
    return values * cosine + swapped * jnp.where(is_first, -direction, direction) * sine_tab


def head_probs(q_head, k_head, mask):
    scores = jnp.where(mask, times_transposed(q_head, k_head) * SCALE, -1e30)
    log_total = jnp.log(jnp.sum(jnp.exp(scores), axis=-1, keepdims=True))
    return jnp.exp(scores - log_total)


def attend_kernel(width, qkv_ref, cos_ref, sin_ref, mask_ref, rot_ref, att_ref):
    cosine, sine_tab = cos_ref[...], sin_ref[...]
    mask = mask_ref[0] > 0.5
    lanes = 2 * HEAD_DIM
    for at in range(0, width, lanes):
        q_two = turn(qkv_ref[:, at : at + lanes], cosine, sine_tab, 1.0).astype(jnp.bfloat16)
        k_at, v_at = width + at, 2 * width + at
        k_two = turn(qkv_ref[:, k_at : k_at + lanes], cosine, sine_tab, 1.0).astype(jnp.bfloat16)
        v_two = qkv_ref[:, v_at : v_at + lanes].astype(jnp.bfloat16)
        rot_ref[:, at : at + lanes] = q_two
        rot_ref[:, k_at : k_at + lanes] = k_two
        rot_ref[:, v_at : v_at + lanes] = v_two
        mixed = []
        for h in range(0, lanes, HEAD_DIM):
            one = slice(h, h + HEAD_DIM)
            probs = head_probs(q_two[:, one], k_two[:, one], mask).astype(jnp.bfloat16)
            mixed.append(times_plain(probs, v_two[:, one]))
        att_ref[:, at : at + lanes] = jnp.concatenate(mixed, axis=1).astype(att_ref.dtype)


def attend_back_kernel(width, rot_ref, g_ref, cos_ref, sin_ref, mask_ref, back_ref):
    cosine, sine_tab = cos_ref[...], sin_ref[...]
    mask = mask_ref[0] > 0.5
    lanes = 2 * HEAD_DIM
    for at in range(0, width, lanes):
        k_at, v_at = width + at, 2 * width + at
        q_two = rot_ref[:, at : at + lanes]
        k_two = rot_ref[:, k_at : k_at + lanes]
        v_two = rot_ref[:, v_at : v_at + lanes]
        g_two = g_ref[:, at : at + lanes]
        grads = ([], [], [])
        for h in range(0, lanes, HEAD_DIM):
            one = slice(h, h + HEAD_DIM)
            q, k, v, g = q_two[:, one], k_two[:, one], v_two[:, one], g_two[:, one]
            probs = head_probs(q, k, mask)
            grad_probs = times_transposed(g, v)
            inner = jnp.sum(probs * grad_probs, axis=-1, keepdims=True)
            grad_scores = (probs * (grad_probs - inner) * SCALE).astype(jnp.bfloat16)
            grads[0].append(times_plain(grad_scores, k))
            grads[1].append(token_contract(grad_scores, q))
            grads[2].append(token_contract(probs.astype(jnp.bfloat16), g))
        grad_q, grad_k, grad_v = (jnp.concatenate(g, axis=1) for g in grads)
        dtype = back_ref.dtype
        back_ref[:, at : at + lanes] = turn(grad_q, cosine, sine_tab, -1.0).astype(dtype)
        back_ref[:, k_at : k_at + lanes] = turn(grad_k, cosine, sine_tab, -1.0).astype(dtype)
        back_ref[:, v_at : v_at + lanes] = grad_v.astype(dtype)


def pack_specs(length, *widths):
    return [pl.BlockSpec((length, width), lambda i: (i, 0)) for width in widths]


def wide_tables(segment_rows):
    cosine, sine_tab = positions_tables(segment_rows, HEAD_DIM)
    mask = allowed(segment_rows).astype(jnp.float32)
    return jnp.tile(cosine, (1, 4)), jnp.tile(sine_tab, (1, 4)), mask


def attend(qkv, tables):
    cosine, sine_tab, mask = tables
    packs, length, _ = mask.shape
    tokens, width = qkv.shape[0], qkv.shape[1] // 3
    return pl.pallas_call(
        functools.partial(attend_kernel, width),
        grid=(packs,),
        out_shape=[
            jax.ShapeDtypeStruct((tokens, 3 * width), jnp.bfloat16),
            jax.ShapeDtypeStruct((tokens, width), jnp.bfloat16),
        ],
        in_specs=pack_specs(length, 3 * width, 2 * HEAD_DIM, 2 * HEAD_DIM)
        + [pl.BlockSpec((1, length, length), lambda i: (i, 0, 0))],
        out_specs=pack_specs(length, 3 * width, width),
        name="attend",
    )(qkv, cosine, sine_tab, mask)


def attend_back(rotated, grad_att, tables):
    cosine, sine_tab, mask = tables
    packs, length, _ = mask.shape
    tokens, width = grad_att.shape
    return pl.pallas_call(
        functools.partial(attend_back_kernel, width),
        grid=(packs,),
        out_shape=jax.ShapeDtypeStruct((tokens, 3 * width), jnp.bfloat16),
        in_specs=pack_specs(length, 3 * width, width, 2 * HEAD_DIM, 2 * HEAD_DIM)
        + [pl.BlockSpec((1, length, length), lambda i: (i, 0, 0))],
        out_specs=pack_specs(length, 3 * width)[0],
        name="attend_back",
    )(rotated, grad_att, cosine, sine_tab, mask)


def attend_plain(qkv, segment_rows):
    width = qkv.shape[1] // 3
    cosine, sine_tab = positions_tables(segment_rows, HEAD_DIM)
    q_rot = rotate(qkv[:, :width], cosine, sine_tab, 1.0, HEAD_DIM).astype(jnp.bfloat16)
    k_rot = rotate(qkv[:, width : 2 * width], cosine, sine_tab, 1.0, HEAD_DIM).astype(jnp.bfloat16)
    v_vals = qkv[:, 2 * width :].astype(jnp.bfloat16)
    attended, log_total = attention_forward(q_rot, k_rot, v_vals, segment_rows, HEAD_DIM)
    return (q_rot, k_rot, v_vals, log_total), attended


def attend_back_plain(rotated, grad_att, segment_rows):
    cosine, sine_tab = positions_tables(segment_rows, HEAD_DIM)
    q_rot, k_rot, v_vals, log_total = rotated
    grad_q, grad_k, grad_v = attention_backward(
        q_rot, k_rot, v_vals, log_total, grad_att, segment_rows, HEAD_DIM
    )
    q_back = rotate(grad_q, cosine, sine_tab, -1.0, HEAD_DIM)
    k_back = rotate(grad_k, cosine, sine_tab, -1.0, HEAD_DIM)
    return jnp.concatenate([q_back, k_back, grad_v], axis=1).astype(jnp.bfloat16)


def norm_scale(values):
    return lax.rsqrt(jnp.mean(values * values, axis=-1, keepdims=True) + EPS)


def norm_back(upstream, source, scale, gain, grad_normed):
    gain_term = jnp.sum(grad_normed * source * scale, axis=0)
    weighted = gain * grad_normed
    grad = (
        upstream
        + scale * weighted
        - source * (scale * scale * scale) * jnp.mean(weighted * source, axis=-1, keepdims=True)
    )
    return grad, gain_term


def per_device(
    block_input,
    segment_ids,
    attn_gain,
    mlp_gain,
    w_query,
    w_key,
    w_value,
    w_out,
    w_gate,
    w_up,
    w_down,
    out_grad,
):
    n = lax.axis_size("shard")
    row_count, model_width = block_input.shape

    def spread(x):
        return gather_rows(x).reshape(n * row_count, -1)

    def collect(partial):
        return scatter_rows(partial.astype(jnp.bfloat16).reshape(n, row_count, model_width))

    gains, segment_rows = gather_small(jnp.stack([attn_gain, mlp_gain]), segment_ids)
    gain_one, gain_two = gains[0].astype(jnp.float32), gains[1].astype(jnp.float32)
    qkv_cols = to_columns((w_query, w_key, w_value))
    pair_cols = to_columns((w_gate, w_up))
    head_width, ff_width = qkv_cols.shape[1] // 3, pair_cols.shape[1] // 2
    gate_cols, up_cols = pair_cols[:, :ff_width], pair_cols[:, ff_width:]
    by_kernel = head_width % (2 * HEAD_DIM) == 0

    input_f = block_input.astype(jnp.float32)
    scale_one = norm_scale(input_f)
    normed_one = spread((input_f * scale_one * gain_one).astype(jnp.bfloat16))
    cotangent = lax.all_gather(after(out_grad, normed_one), "shard", axis=0, tiled=True)
    qkv = times_plain(normed_one, qkv_cols)
    if by_kernel:
        tables = wide_tables(segment_rows)
        rotated, attended = attend(qkv, tables)
    else:
        rotated, attended = attend_plain(qkv, segment_rows)
    residual = input_f + collect(times_plain(attended, w_out))
    scale_two = norm_scale(residual)
    normed_two = spread((residual * scale_two * gain_two).astype(jnp.bfloat16))
    gate_pre = times_plain(normed_two, gate_cols)
    up_pre = times_plain(normed_two, up_cols)
    gate_sig = jax.nn.sigmoid(gate_pre)
    silu_val = gate_pre * gate_sig
    hidden_b = (silu_val * up_pre).astype(jnp.bfloat16)
    block_output = (residual + collect(times_plain(hidden_b, w_down))).astype(jnp.bfloat16)

    grad_hidden = times_transposed(cotangent, w_down)
    gate_b = (grad_hidden * up_pre * gate_sig * (1.0 + gate_pre * (1.0 - gate_sig))).astype(
        jnp.bfloat16
    )
    up_b = (grad_hidden * silu_val).astype(jnp.bfloat16)
    pair_b = jnp.concatenate([gate_b, up_b], axis=1)
    pair_sum = sum_copies(token_contract(normed_two, pair_b).astype(jnp.bfloat16))
    grad_down = token_contract(hidden_b, cotangent).astype(jnp.bfloat16)
    grad_down = lax.psum(after(grad_down, pair_sum), "replica")
    grad_normed_two = collect(times_transposed(pair_b, pair_cols))
    grad_residual, gain_two_term = norm_back(
        out_grad.astype(jnp.float32), residual, scale_two, gain_two, grad_normed_two
    )
    residual_b = spread(grad_residual.astype(jnp.bfloat16))
    grad_gate, grad_up = to_rows(after(pair_sum, residual_b), (ff_width, ff_width))
    grad_out = token_contract(attended, residual_b).astype(jnp.bfloat16)
    grad_out = lax.psum(after(grad_out, grad_down), "replica")
    grad_att = times_transposed(residual_b, w_out).astype(jnp.bfloat16)
    if by_kernel:
        back = attend_back(rotated, grad_att, tables)
    else:
        back = attend_back_plain(rotated, grad_att, segment_rows)
    qkv_sum = sum_copies(
        after(token_contract(normed_one, back).astype(jnp.bfloat16), grad_out)
    )
    grad_normed_one = collect(times_transposed(back, qkv_cols))
    input_grad, gain_one_term = norm_back(
        grad_residual, input_f, scale_one, gain_one, grad_normed_one
    )
    gain_rows = sum_small(jnp.stack([gain_one_term, gain_two_term]))
    grad_query, grad_key, grad_value = to_rows(
        after(qkv_sum, grad_normed_one), (head_width,) * 3
    )
    return (
        block_output,
        input_grad,
        grad_query,
        grad_key,
        grad_value,
        grad_out.astype(jnp.float32),
        grad_gate,
        grad_up,
        grad_down.astype(jnp.float32),
        gain_rows[0],
        gain_rows[1],
    )


def solution(mesh):
    placed = (
        P(("replica", "shard"), None),
        P(("replica", "shard"), None),
        P("shard"),
        P("shard"),
        P("shard", None),
        P("shard", None),
        P("shard", None),
        P("shard", None),
        P("shard", None),
        P("shard", None),
        P("shard", None),
        P(("replica", "shard"), None),
    )
    return jax.shard_map(
        per_device,
        mesh=mesh,
        in_specs=placed,
        out_specs=(
            P(("replica", "shard"), None),
            P(("replica", "shard"), None),
            P("shard", None),
            P("shard", None),
            P("shard", None),
            P("shard", None),
            P("shard", None),
            P("shard", None),
            P("shard", None),
            P("shard"),
            P("shard"),
        ),
        check_vma=False,
    )
```

time: 5090 us -> 1210 us (0.24)
  waiting for transfers between devices: 4650 us -> 50.8 us
  Pallas kernels: 0 us -> 691 us
  matrix products: 292 us -> 180 us
  blocking collectives: 80.8 us -> 188 us
    all_gather x7 -> x5, waiting for transfers between devices: 2290 us -> 25.1 us  [the longest x2 25.1 us: to_rows(): lax.all_gather(swapped, 'replica', axis=0, tiled=False)]
    reduce_scatter x7 -> x2, waiting for transfers between devices: 2150 us -> 0.02 us  [sum_copies(): return lax.psum_scatter(split, 'replica', scatter_dimension=0, tiled=False)]
    pallas_call x0 -> x13, Pallas kernels: none -> 691 us  [the longest x4 371 us: scatter_rows(): pl.pallas_call(functools.partial(scatter_kernel, n, across, chunks), out_...]
    all_to_all x0 -> x4, blocking collectives: none -> 188 us  [the longest x2 111 us: to_columns(): lax.all_to_all(jnp.concatenate(pieces, axis=2), 'shard', split_axis=0, co...]
    psum x1 -> x2, waiting for transfers between devices: 212 us -> 25.5 us  [the longest x1 25.5 us: per_device(): grad_out = lax.psum(after(grad_out, grad_down), 'replica')]
  transfers between devices with their start and end apart: 15 -> 9, of which waited for: 15 -> 2; matrix products, arithmetic and copies ran while one was open for 4% -> 14% of each run, Pallas kernels for 0% -> 57%
where the time goes in v1:
time: 1210 us; the launch traced here: 1200 us
  Pallas kernels  691 us (57%)
  blocking collectives  188 us (16%)
  matrix products  180 us (15%)
  waiting for transfers between devices  50.8 us (4%)
  local copies, waits for them, and re-layouts  47.4 us (4%)
  other arithmetic  30.8 us (3%)
  between operations  14.6 us (1%)
    pallas_call x4, Pallas kernels, scatter_rows(): pl.pallas_call(functools.partial(scatter_kernel, n, across, chunks), out_...  371 us
    pallas_call x3, Pallas kernels, gather_rows(): pl.pallas_call(functools.partial(gather_kernel, n, across, chunks), out_s...  249 us
    all_to_all x2, blocking collectives, to_columns(): lax.all_to_all(jnp.concatenate(pieces, axis=2), 'shard', split_axis=0, co...  111 us
    all_to_all x2, blocking collectives, to_rows(): lax.all_to_all(summed, 'shard', split_axis=0, concat_axis=0, tiled=True)  76.5 us
    dot_general x5, matrix products, times_plain(): return jnp.dot(left_op, right_op, preferred_element_type=jnp.float32)  69.3 us
    dot_general x4, matrix products, times_transposed(): lax.dot_general(left_op, right_op, (((1,), (1,)), ((), ())), preferred_el...  56.3 us
    dot_general x4, matrix products, token_contract(): lax.dot_general(left_op, right_op, (((0,), (0,)), ((), ())), preferred_el...  54.4 us
    psum x1, waiting for transfers between devices, per_device(): grad_out = lax.psum(after(grad_out, grad_down), 'replica')  25.5 us
  transfers between devices with their start and end apart: 9, of which 2 were waited for; matrix products, arithmetic and copies ran while one was open for 14% of the time, Pallas kernels for 57%

profile of v1, /device:TPU:0, one launch (start us, length us, event | category | flops | bytes accessed | tf_op | source)
XLA Modules:
  0.0 1203.6 jit_solution(12970342735722234214)
XLA Ops:
  9.8 27.3 %all_to_all.20 = bf16[8,64,768]{2,1,0:T(8,128)(2,1)S(1)} all-to-all(bf16[8,64,768]{2,1,0:T(8,128)(2,1)S(1)} %copy.41), channel_id=1, replica_groups=mesh['replica'=4,'shard'=8] {'shard'}, dimensions={0} | all-to-all | bytes 1572864 | tf_op jit(solution)/shard_map/all_to_all | solution.py:563
  39.7 8.1 gather_small.1
  51.4 83.4 %gather_rows.3 = bf16[8,256,2048]{2,1,0:T(8,128)(2,1)} custom-call(bf16[256,2048]{1,0:T(8,128)(2,1)} %fusion.7.x_ref), custom_call_target="tpu_custom_call" | custom-call | bytes 251658240 | tf_op jit(solution)/shard_map/gather_rows/pallas_call | solution.py:234
  139.2 84.2 %all_to_all.21 = bf16[8,64,2048]{2,1,0:T(8,128)(2,1)S(1)} all-to-all(bf16[8,64,2048]{2,1,0:T(8,128)(2,1)S(1)} %copy.47), channel_id=1, replica_groups=mesh['replica'=4,'shard'=8] {'shard'}, dimensions={0} | all-to-all | bytes 4194304 | tf_op jit(solution)/shard_map/all_to_all | solution.py:563
  237.8 10.8 fusion.22.qkv_ref
  248.6 12.4 %attend.1 = (bf16[2048,768]{1,0:T(8,128)(2,1)}, bf16[2048,256]{1,0:T(8,128)(2,1)}) custom-call(f32[2048,768]{1,0:T(8,128)} %fusion.22.qkv_ref, f32[2048,128]{1,0:T(8,128)} %copy.45.cos_ref, f32[2048,128]{1,0:T(8,128)} %copy.46.sin_ref, f32[8,256,256]{2,1,0:T(8,128)} %and_convert_fusion.mask_ref), custom_call_target="tpu_custom_call" | custom-call | tf_op jit(solution)/shard_map/attend/pallas_call | solution.py:778
  260.9 7.0 convolution_convert_fusion.4
  267.9 111.1 %scatter_rows.4 = f32[256,2048]{1,0:T(8,128)} custom-call(bf16[8,256,2048]{2,1,0:T(8,128)(2,1)} %bitcast.88), custom_call_target="tpu_custom_call" | custom-call | bytes 251658240 | tf_op jit(solution)/shard_map/scatter_rows/pallas_call | solution.py:422
  383.5 83.1 %gather_rows.4 = bf16[8,256,2048]{2,1,0:T(8,128)(2,1)} custom-call(bf16[256,2048]{1,0:T(8,128)(2,1)} %multiply_convert_fusion.3.x_ref), custom_call_target="tpu_custom_call" | custom-call | bytes 251658240 | tf_op jit(solution)/shard_map/gather_rows/pallas_call | solution.py:234
  466.7 14.6 %fusion.23 = f32[2048,1024]{0,1:T(8,128)} fusion(bf16[2048,2048]{1,0:T(8,128)(2,1)} %all-gather.10.cloned.1.call-done, bf16[1024,2048]{1,0:T(8,128)(2,1)} %param.22), kind=kOutput, calls=%fused_computation.80 | convolution fusion | flops 8589934592 | bytes 20971520 | tf_op jit(solution)/shard_map/dot_general | solution.py:26
  481.2 11.4 copy.49
  492.6 15.0 %fusion.1 = f32[2048,1024]{0,1:T(8,128)} fusion(bf16[2048,2048]{1,0:T(8,128)(2,1)} %bitcast.96, bf16[2048,2048]{1,0:T(8,128)(2,1)} %bitcast.100), kind=kOutput, calls=%fused_computation.18 | convolution fusion | flops 8589934592 | bytes 20971520 | tf_op jit(solution)/shard_map/dot_general | solution.py:22
  507.6 22.5 %multiply_convert_fusion.1 = (bf16[2048,1024]{0,1:T(8,128)(2,1)}, bf16[2048,1024]{0,1:T(8,128)(2,1)}, bf16[2048,1024]{0,1:T(8,128)(2,1)}) fusion(f32[2048,1024]{0,1:T(8,128)} %fusion.23, f32[2048,1024]{0,1:T(8,128)} %fusion.1, bf16[2048,2048]{1,0:T(8,128)(2,1)} %bitcast.97, bf16[2048,2048]{1,0:T(8,128)(2,1)} %bitcast.101), kind=kOutput, calls=%fused_computation.3 | convolution fusion | flops 8621391872 | bytes 41943040 | tf_op jit(solution)/shard_map/dot_general | solution.py:22
  530.2 23.8 %convolution_convert_fusion = bf16[2048,2048]{1,0:T(8,128)(2,1)} fusion(bf16[2048,2048]{1,0:T(8,128)(2,1)} %bitcast.98, bf16[2048,1024]{0,1:T(8,128)(2,1)} %get-tuple-element.50, bf16[2048,1024]{0,1:T(8,128)(2,1)} %get-tuple-element.49), kind=kOutput, calls=%fused_computation.7 | convolution fusion | flops 17200840704 | bytes 25165824 | tf_op jit(solution)/shard_map/dot_general | solution.py:32
  554.0 8.4 copy.64
  562.5 23.7 %convolution_convert_fusion.2 = bf16[2048,2048]{1,0:T(8,128)(2,1)} fusion(bf16[2048,2048]{1,0:T(8,128)(2,1)} %bitcast.102, bf16[2048,1024]{0,1:T(8,128)(2,1)} %get-tuple-element.50, bf16[2048,1024]{0,1:T(8,128)(2,1)} %get-tuple-element.49), kind=kOutput, calls=%fused_computation.9 | convolution fusion | flops 17200840704 | bytes 25165824 | tf_op jit(solution)/shard_map/dot_general | solution.py:26
  586.2 85.9 %scatter_rows.6 = f32[256,2048]{1,0:T(8,128)} custom-call(bf16[8,256,2048]{2,1,0:T(8,128)(2,1)} %bitcast.91), custom_call_target="tpu_custom_call" | custom-call | bytes 251658240 | tf_op jit(solution)/shard_map/scatter_rows/pallas_call | solution.py:422
  672.1 14.0 %convolution_convert_fusion.3 = bf16[2048,2048]{1,0:T(8,128)(2,1)} fusion(bf16[2048,1024]{0,1:T(8,128)(2,1)} %get-tuple-element.51, bf16[1024,2048]{1,0:T(8,128)(2,1)} %param.22), kind=kOutput, calls=%fused_computation.10 | convolution fusion | flops 8594128896 | bytes 16777216 | tf_op jit(solution)/shard_map/dot_general | solution.py:22
  686.1 86.4 %scatter_rows.5 = f32[256,2048]{1,0:T(8,128)} custom-call(bf16[8,256,2048]{2,1,0:T(8,128)(2,1)} %bitcast.93), custom_call_target="tpu_custom_call" | custom-call | bytes 251658240 | tf_op jit(solution)/shard_map/scatter_rows/pallas_call | solution.py:422
  775.4 12.5 %convolution_convert_fusion.5 = bf16[1024,2048]{1,0:T(8,128)(2,1)} fusion(bf16[2048,1024]{0,1:T(8,128)(2,1)S(1)} %copy-done.22, bf16[2048,2048]{1,0:T(8,128)(2,1)} %all-gather.10.cloned.1.call-done), kind=kOutput, calls=%fused_computation.22 | convolution fusion | flops 8592031744 | bytes 16777216 | tf_op jit(solution)/shard_map/dot_general | solution.py:32
  793.9 83.0 %gather_rows.5 = bf16[8,256,2048]{2,1,0:T(8,128)(2,1)} custom-call(bf16[256,2048]{1,0:T(8,128)(2,1)} %get-tuple-element.45.x_ref), custom_call_target="tpu_custom_call" | custom-call | bytes 251658240 | tf_op jit(solution)/shard_map/gather_rows/pallas_call | solution.py:234
  876.8 6.7 convolution_convert_fusion.8.g_ref
  883.6 22.0 %attend_back.1 = bf16[2048,768]{1,0:T(8,128)(2,1)} custom-call(bf16[2048,768]{1,0:T(8,128)(2,1)} %get-tuple-element.30.rot_ref, bf16[2048,256]{1,0:T(8,128)(2,1)} %convolution_convert_fusion.8.g_ref, f32[2048,128]{1,0:T(8,128)} %copy.45.cos_ref, f32[2048,128]{1,0:T(8,128)} %copy.46.sin_ref, f32[8,256,256]{2,1,0:T(8,128)} %and_convert_fusion.mask_ref), custom_call_target="tpu_custom_call" | custom-call | tf_op jit(solution)/shard_map/attend_back/pallas_call | solution.py:796
  912.4 11.4 convolution_convert_fusion.6
  923.7 25.5 %all-reduce.8.cloned.1.call-done = bf16[256,2048]{1,0:T(8,128)(2,1)} async-done(((bf16[256,2048]{1,0:T(8,128)(2,1)}), bf16[256,2048]{1,0:T(8,128)(2,1)}) %all-reduce.8.cloned.1.call-update) | async-done | bytes 1048592 | tf_op jit(solution)/shard_map/psum | solution.py:910
  953.4 11.4 convolution_convert_fusion.1
  964.8 87.5 %scatter_rows.7 = f32[256,2048]{1,0:T(8,128)} custom-call(bf16[8,256,2048]{2,1,0:T(8,128)(2,1)} %bitcast.92), custom_call_target="tpu_custom_call" | custom-call | bytes 251658240 | tf_op jit(solution)/shard_map/scatter_rows/pallas_call | solution.py:422
  1052.3 24.7 %all_to_all.22 = bf16[8,64,768]{2,1,0:T(8,128)(2,1)} all-to-all(bf16[8,64,768]{2,1,0:T(8,128)(2,1)} %bitcast.121), channel_id=1, replica_groups=mesh['replica'=4,'shard'=8] {'shard'}, dimensions={0} | all-to-all | bytes 1572864 | tf_op jit(solution)/shard_map/all_to_all | solution.py:587
  1077.1 51.8 %all_to_all.23 = bf16[8,64,2048]{2,1,0:T(8,128)(2,1)} all-to-all(bf16[8,64,2048]{2,1,0:T(8,128)(2,1)} %bitcast.114), channel_id=1, replica_groups=mesh['replica'=4,'shard'=8] {'shard'}, dimensions={0} | all-to-all | bytes 4194304 | tf_op jit(solution)/shard_map/all_to_all | solution.py:587
  1131.7 11.7 sum_small.1
  1161.6 25.1 %all-gather.18.cloned.1.call-done = bf16[32,64,2048]{2,1,0:T(8,128)(2,1)} async-done(((bf16[8,64,2048]{2,1,0:T(8,128)(2,1)}), bf16[32,64,2048]{2,1,0:T(8,128)(2,1)}) %all-gather.18.cloned.1.call-update) | async-done | bytes 8388624 | tf_op jit(solution)/shard_map/all_gather | solution.py:588
  1186.7 10.1 unpack.3
  (132 shorter events, 72.5 us)
Async XLA Ops:
  7.2 253.8 %copy-start = (bf16[256,2048]{1,0:T(8,128)(2,1)S(1)}, bf16[256,2048]{1,0:T(8,128)(2,1)}, u32[]{:S(2)}) copy-start(bf16[256,2048]{1,0:T(8,128)(2,1)} %param.19) | copy-start | bytes 3145732
  7.2 226.5 %all-gather.12.cloned.1.call-start = ((), (), s32[]{:S(2)}) async-start(), calls=%async_computation.11 | async-start | bytes 3932160 | tf_op jit(solution)/shard_map/all_gather | solution.py:566
  9.4 29.0 %copy-start.20 = (bf16[256]{0:T(256)(128)(2,1)S(1)}, bf16[256]{0:T(256)(128)(2,1)}, u32[]{:S(2)}) copy-start(bf16[256]{0:T(256)(128)(2,1)} %param.14) | copy-start | bytes 1540
  9.4 29.0 %copy-start.21 = (bf16[256]{0:T(256)(128)(2,1)S(1)}, bf16[256]{0:T(256)(128)(2,1)}, u32[]{:S(2)}) copy-start(bf16[256]{0:T(256)(128)(2,1)} %param.15) | copy-start | bytes 1540
  9.5 29.6 %copy-start.19 = (s32[1,256]{1,0:T(1,128)S(1)}, s32[1,256]{1,0:T(1,128)}, u32[]{:S(2)}) copy-start(s32[1,256]{1,0:T(1,128)} %param.13) | copy-start | bytes 3076
  9.5 38.3 %copy-start.3 = (bf16[256,2048]{1,0:T(8,128)(2,1)S(1)}, bf16[256,2048]{1,0:T(8,128)(2,1)}, u32[]{:S(2)}) copy-start(bf16[256,2048]{1,0:T(8,128)(2,1)} %param.12) | copy-start | bytes 3145732
  38.4 428.3 %all-gather.10.cloned.1.call-start = ((), (), s32[]{:S(2)}) async-start(), calls=%async_computation.6 | async-start | bytes 9437184 | tf_op jit(solution)/shard_map/all_gather | solution.py:877
  48.7 86.2 %copy-start.13 = (f32[256]{0:T(256)}, f32[256]{0:T(256)S(1)}, u32[]{:S(2)}) copy-start(f32[256]{0:T(256)S(1)} %get-tuple-element.60) | copy-start | bytes 3076
  49.6 0.6 copy-start.9
  49.6 332.0 %copy-start.11 = (f32[1,8,256]{2,0,1:T(1,128)}, f32[1,8,256]{2,0,1:T(1,128)S(1)}, u32[]{:S(2)}) copy-start(f32[1,8,256]{2,0,1:T(1,128)S(1)} %get-tuple-element.53) | copy-start | bytes 24580
  134.9 346.3 %all-gather.14.cloned.1.call-start = ((), (), s32[]{:S(2)}) async-start(), calls=%async_computation.12 | async-start | bytes 10485760 | tf_op jit(solution)/shard_map/all_gather | solution.py:566
  225.9 561.9 %reduce-scatter.3.cloned.1.call-start = ((), (), s32[]{:S(2)}) async-start(), calls=%async_computation.7 | async-start | bytes 10485760 | tf_op jit(solution)/shard_map/reduce_scatter | solution.py:574
  236.2 1.6 copy-start.7
  381.0 1.3 copy-start.1
  381.6 0.7 copy-start.15
  562.5 349.8 %all-reduce.6.cloned.1.call-start = ((), (), s32[]{:S(2)}) async-start(), calls=%async_computation.8 | async-start | bytes 8388608 | tf_op jit(solution)/shard_map/psum | solution.py:902
  686.1 86.4 %copy-start.2 = (f32[256,2048]{1,0:T(8,128)S(1)}, f32[256,2048]{1,0:T(8,128)}, u32[]{:S(2)}) copy-start(f32[256,2048]{1,0:T(8,128)} %copy-done.1) | copy-start | bytes 6291460
  686.1 86.4 %copy-start.12 = (f32[1,8,256]{2,0,1:T(1,128)S(1)}, f32[1,8,256]{2,0,1:T(1,128)}, u32[]{:S(2)}) copy-start(f32[1,8,256]{2,0,1:T(1,128)} %copy-done.11) | copy-start | bytes 24580
  686.1 86.4 %copy-start.16 = (f32[256]{0:T(256)S(1)}, f32[256]{0:T(256)}, u32[]{:S(2)}) copy-start(f32[256]{0:T(256)} %copy-done.15) | copy-start | bytes 3076
  772.5 2.8 copy-start.22
  787.9 0.7 copy-start.18
  787.9 161.3 %all-reduce.8.cloned.1.call-start = ((), (), s32[]{:S(2)}) async-start(), calls=%async_computation.9 | async-start | bytes 2097152 | tf_op jit(solution)/shard_map/psum | solution.py:910
  883.6 22.0 %copy-start.5 = (bf16[2048,256]{1,0:T(8,128)(2,1)S(1)}, bf16[2048,256]{1,0:T(8,128)(2,1)}, u32[]{:S(2)}) copy-start(bf16[2048,256]{1,0:T(8,128)(2,1)} %get-tuple-element.28) | copy-start | bytes 3145732
  912.3 139.9 %reduce-scatter.5.cloned.1.call-start = ((), (), s32[]{:S(2)}) async-start(), calls=%async_computation.10 | async-start | bytes 3932160 | tf_op jit(solution)/shard_map/reduce_scatter | solution.py:574
  953.1 201.9 %all-gather.16.cloned.1.call-start = ((), (), s32[]{:S(2)}) async-start(), calls=%async_computation.13 | async-start | bytes 3932160 | tf_op jit(solution)/shard_map/all_gather | solution.py:588
  1052.2 76.6 %copy-start.4 = (bf16[256,2048]{1,0:T(8,128)(2,1)S(1)}, bf16[256,2048]{1,0:T(8,128)(2,1)}, u32[]{:S(2)}) copy-start(bf16[256,2048]{1,0:T(8,128)(2,1)} %param.12) | copy-start | bytes 3145732
  1052.3 76.6 %copy-start.10 = (f32[1,8,256]{2,0,1:T(1,128)S(1)}, f32[1,8,256]{2,0,1:T(1,128)}, u32[]{:S(2)}) copy-start(f32[1,8,256]{2,0,1:T(1,128)} %copy-done.9) | copy-start | bytes 24580
  1052.3 76.6 %copy-start.14 = (f32[256]{0:T(256)S(1)}, f32[256]{0:T(256)}, u32[]{:S(2)}) copy-start(f32[256]{0:T(256)} %copy-done.13) | copy-start | bytes 3076
  1077.0 67.9 %copy-start.17 = (f32[256]{0:T(256)S(1)}, f32[256]{0:T(256)}, u32[]{:S(2)}) copy-start(f32[256]{0:T(256)} %get-tuple-element.59) | copy-start | bytes 3076
  1077.0 109.7 %all-gather.18.cloned.1.call-start = ((), (), s32[]{:S(2)}) async-start(), calls=%async_computation.14 | async-start | bytes 10485760 | tf_op jit(solution)/shard_map/all_gather | solution.py:588
  1143.4 5.6 copy-start.6
  1149.0 4.5 copy-start.8
Sparse Core Ops, SparseCore 0:
  38.5 27.5 all-gather.11
  135.0 180.6 all-gather.9
  317.9 60.3 all-gather.13
  562.6 70.8 reduce-scatter.2
  788.0 86.6 all-reduce.5
  912.4 36.7 all-reduce.7
  953.3 38.3 reduce-scatter.4
  1077.1 27.3 all-gather.15
  1129.0 57.6 all-gather.17
